TPU v7x, 8 devices: a whole 2x2x1 slice. The times are simulated.
8 devices in a mesh: dp: 2 (over z, y), tp: 4 (over x, core).
Axes of the slice: x: 2, y: 2, z: 1, core: 2. Of those that a mesh axis runs over, the one named last changes fastest.
Arguments:
- x_in: bfloat16 [2, 128, 5120], P('dp', 'tp'), parts along dimension 0
- ln1_gain: float32 [2, 5120], replicated
- w_qkv: bfloat16 [2, 5120, 40, 384], P(None, None, 'tp')
- w_out: bfloat16 [2, 40, 128, 5120], P(None, 'tp')
- ln2_gain: float32 [2, 5120], replicated
- w_up: bfloat16 [2, 5120, 20480], P(None, None, 'tp')
- w_down: bfloat16 [2, 20480, 5120], P(None, 'tp')
Outputs:
- output: bfloat16 [2, 128, 5120], P('dp', 'tp'), parts along dimension 0
There are 2 independent parts. A program takes and returns all parts, laid end to end along the dimension named above; an argument that names none is the same for every part.
All inputs are finite; a program needn't handle non-finite values.
Results may differ from a plain program's by a relative error of at most 0.02.
Values are sent between devices in bfloat16 or wider.
A program may use at most 1.25 GiB of HBM per device.

v0:
```python
import functools

import jax
import jax.numpy as jnp
from jax import lax
from jax.experimental import pallas as pl
from jax.experimental.pallas import tpu as pltpu
from jax.sharding import PartitionSpec as P

LN_EPS = 1.0e-5
NEG_BIG = -1.0e30
MESH = pl.DeviceIdType.MESH

TP = 4
SEQ = 128
ROWS = SEQ // TP
D = 5120
C = 1280
NC = D // C
HEADS = 10
HD = 128
SLOTS = 17
TILES = 48
LAYERS = 2
NW = 256


def stack_kernel(x_hbm, g1_hbm, wqkv_hbm, wout_hbm, g2_hbm, wup_hbm, wdown_hbm, y_hbm,
                 ring, x_all, a_buf, stat, q_stat, mean_b, scale_b, hid, acc, p_snd, p_rcv, q_snd, q_rcv, g1_ref, g2_ref,
                 ring_sem, x_sem, g_sem, ag_s, ag_r, st_s, st_r, p_s, p_r, q_s, q_r):
    me = lax.axis_index('tp')
    partner = me + 1 - 2 * lax.rem(me, 2)
    cross = lax.rem(me + 2, TP)
    diag = lax.rem(partner + 2, TP)

    def slot_of(layer, i):
        return lax.rem(TILES * layer + i, SLOTS)

    def tile(w, layer, row, col, slot):
        rows = pl.ds(pl.multiple_of(row * C, C), C)
        cols = pl.ds(pl.multiple_of(col * C, C), C)
        return pltpu.make_async_copy(w.at[layer, rows, cols], ring.at[slot], ring_sem.at[slot])

    def start_qkv(layer, i):
        j, s = i // 3, i % 3
        slot = slot_of(layer, i)
        rows = pl.ds(j * C, C)
        pieces, col = [], 0
        for head in range(HEADS):
            lo, hi = head * 3 * HD, (head + 1) * 3 * HD
            a, b = max(lo, s * C), min(hi, (s + 1) * C)
            if a < b:
                pieces.append((head, a - lo, b - a, a - s * C))
        for head, src, width, dst in pieces:
            pltpu.make_async_copy(wqkv_hbm.at[layer, head, rows, pl.ds(src, width)],
                                  ring.at[slot, :, pl.ds(dst, width)], ring_sem.at[slot]).start(priority=1)

    def start_attention_tile(layer, i):
        if i < 12:
            start_qkv(layer, i)
        else:
            tile(wout_hbm, layer, 0, i - 12, slot_of(layer, i)).start(priority=1)

    def start_up(layer, i):
        tile(wup_hbm, layer, i // NC, lax.rem(i, NC), slot_of(layer, 16 + i)).start(priority=1)

    def start_down(layer, i):
        tile(wdown_hbm, layer, lax.rem(i, NC), i // NC, slot_of(layer, 32 + i)).start(priority=1)

    def wait_tile(layer, i):
        tile(wup_hbm, 0, 0, 0, slot_of(layer, i)).wait()

    def refill(layer, i):
        t = i + SLOTS
        if not isinstance(t, int):
            raise TypeError('static tile')
        if t < 32:
            start_up(layer, t - 16)
        elif t < TILES:
            start_down(layer, t - 32)
        else:
            @pl.when(layer < LAYERS - 1)
            def _():
                if t < TILES + 16:
                    start_attention_tile(layer + 1, t - TILES)
                else:
                    start_up(layer + 1, t - TILES - 16)

    def block(jobs):
        for pairs, dst, add, finish in jobs:
            for n in range(C // NW):
                cols = pl.ds(n * NW, NW)
                part = None
                for lhs, slot in pairs:
                    term = jnp.dot(lhs(), ring[slot, :, cols], preferred_element_type=jnp.float32)
                    part = term if part is None else part + term
                if add:
                    part = part + acc[dst, :, :, cols].reshape(SEQ, NW)
                if finish is None:
                    acc[dst, :, :, cols] = part.reshape(TP, ROWS, NW)
                else:
                    finish(part, dst, cols)

    def remote(src, dst, send_sem, recv_sem, peer):
        return pltpu.make_async_remote_copy(src_ref=src, dst_ref=dst, send_sem=send_sem, recv_sem=recv_sem,
                                            device_id={'tp': peer}, device_id_type=MESH)

    def ag_copy(j, kind):
        source, peer = ((me, partner), (me, cross), (cross, partner))[kind]
        return remote(x_all.at[j, source], x_all.at[j, source], ag_s.at[kind, j], ag_r.at[kind, j], peer)

    def ag_wait(j, kind):
        source = (partner, cross, diag)[kind]
        remote(x_all.at[j, source], x_all.at[j, source], ag_s.at[kind, j], ag_r.at[kind, j], partner).wait_recv()

    def ag_send(j):
        ag_copy(j, 1).start()
        ag_copy(j, 0).start()

    def forward(j):
        ag_wait(j, 1)
        ag_copy(j, 2).start()

    def stat_copy(k):
        return remote(stat.at[me], stat.at[me], st_s.at[k], st_r.at[k], (partner, cross, diag)[k])

    def quarter_stats(j):
        x = x_all[j, me].astype(jnp.float32)
        mean = jnp.sum(x, axis=-1, keepdims=True) / C
        centered = x - mean
        q_stat[j, 0] = jnp.broadcast_to(mean, (ROWS, HD))
        q_stat[j, 1] = jnp.broadcast_to(jnp.sum(centered * centered, axis=-1, keepdims=True), (ROWS, HD))

    def stats_send():
        mean = (q_stat[0, 0] + q_stat[1, 0] + q_stat[2, 0] + q_stat[3, 0]) / NC
        square = jnp.zeros((ROWS, HD), jnp.float32)
        for j in range(NC):
            shift = q_stat[j, 0] - mean
            square += q_stat[j, 1] + C * (shift * shift)
        scale = lax.rsqrt(square / D + LN_EPS)
        lanes = lax.broadcasted_iota(jnp.int32, (8, HD), 1)
        packed = jnp.zeros((8, HD), jnp.float32)
        for i in range(ROWS // 8):
            packed = jnp.where(lanes == i, mean[8 * i:8 * i + 8], packed)
            packed = jnp.where(lanes == 4 + i, scale[8 * i:8 * i + 8], packed)
        stat[me] = packed
        for k in (1, 2, 0):
            stat_copy(k).start()

    def stats_wait():
        for k, source in enumerate((partner, cross, diag)):
            remote(stat.at[source], stat.at[source], st_s.at[k], st_r.at[k], partner).wait_recv()
        for source in range(TP):
            packed = stat[source]
            for i in range(ROWS // 8):
                rows = pl.ds(source * ROWS + 8 * i, 8)
                mean_b[rows] = jnp.broadcast_to(packed[:, i:i + 1], (8, HD))
                scale_b[rows] = jnp.broadcast_to(packed[:, 4 + i:5 + i], (8, HD))

    def ag_drain():
        for j in range(NC):
            for kind in range(3):
                ag_copy(j, kind).wait_send()
        for k in range(3):
            stat_copy(k).wait_send()

    def normalize(j, g_ref, layer):
        mean, scale = mean_b[...], scale_b[...]
        for k in range(C // HD):
            cols = pl.ds(k * HD, HD)
            gains = g_ref[:, pl.ds(pl.multiple_of(j * C + k * HD, HD), HD)]
            gain = jnp.where(layer == 0, gains[0:1], gains[1:2])
            x = x_all[j, :, :, cols].reshape(SEQ, HD).astype(jnp.float32)
            a_buf[:, cols] = ((x - mean) * scale * gain).astype(jnp.bfloat16)

    def when(cond, body):
        if isinstance(cond, bool):
            if cond:
                body()
        else:
            pl.when(cond)(body)

    def rs_p(q):
        return remote(p_snd.at[lax.rem(q, 2)], p_rcv.at[q], p_s.at[q], p_r.at[q], partner)

    def rs_q(q):
        return remote(q_snd.at[lax.rem(q, 2)], q_rcv.at[q], q_s.at[q], q_r.at[q], cross)

    def rs_a(q):
        when(q >= 2, lambda: rs_p(q - 2).wait_send())
        p_snd[lax.rem(q, 2), 0] = acc[q, partner].astype(jnp.bfloat16)
        p_snd[lax.rem(q, 2), 1] = acc[q, diag].astype(jnp.bfloat16)
        rs_p(q).start()

    def rs_b(q):
        rs_p(q).wait_recv()
        when(q >= 2, lambda: rs_q(q - 2).wait_send())
        q_snd[lax.rem(q, 2)] = (acc[q, cross] + p_rcv[q, 1].astype(jnp.float32)).astype(jnp.bfloat16)
        rs_q(q).start()

    def rs_c(q):
        rs_q(q).wait_recv()
        total = acc[q, me] + p_rcv[q, 0].astype(jnp.float32) + q_rcv[q].astype(jnp.float32)
        x_all[q, me] = (x_all[q, me].astype(jnp.float32) + total).astype(jnp.bfloat16)
        quarter_stats(q)

    def rs_drain():
        for q in range(2, NC):
            rs_p(q).wait_send()
            rs_q(q).wait_send()

    def attention():
        keys = lax.broadcasted_iota(jnp.int32, (SEQ, SEQ), 0)
        queries = lax.broadcasted_iota(jnp.int32, (SEQ, SEQ), 1)
        causal = queries >= keys

        def part(block):
            third, col = block * HD // C, block * HD % C
            return acc[third, :, :, pl.ds(col, HD)].reshape(SEQ, HD).astype(jnp.bfloat16)

        for head in range(HEADS):
            query, key = part(3 * head), part(3 * head + 1)
            scores = lax.dot_general(key, query, (((1,), (1,)), ((), ())), preferred_element_type=jnp.float32)
            scores = jnp.where(causal, scores * HD ** -0.5, NEG_BIG)
            acc[3, :, :, pl.ds(head * HD, HD)] = scores.reshape(TP, ROWS, HD)
        for head in range(HEADS):
            scores = acc[3, :, :, pl.ds(head * HD, HD)].reshape(SEQ, SEQ)
            probs = jnp.exp(scores - jnp.max(scores, axis=0, keepdims=True))
            hid[0, :, pl.ds(head * HD, HD)] = (probs / jnp.sum(probs, axis=0, keepdims=True)).astype(jnp.bfloat16)
        for head in range(HEADS):
            out = lax.dot_general(hid[0, :, pl.ds(head * HD, HD)], part(3 * head + 2), (((0,), (0,)), ((), ())),
                                  preferred_element_type=jnp.float32)
            a_buf[:, pl.ds(head * HD, HD)] = out.astype(jnp.bfloat16)

    x_copies = [pltpu.make_async_copy(x_hbm.at[0, :, pl.ds(j * C, C)], x_all.at[j, me], x_sem.at[j]) for j in range(NC)]
    g_copies = [pltpu.make_async_copy(g1_hbm, g1_ref, g_sem.at[0]), pltpu.make_async_copy(g2_hbm, g2_ref, g_sem.at[1])]
    for copy in x_copies + g_copies:
        copy.start()
    for i in range(16):
        start_attention_tile(0, i)
    for i in range(SLOTS - 16):
        start_up(0, i)
    barrier = pltpu.get_barrier_semaphore()
    for peer in (partner, cross, diag):
        pl.semaphore_signal(barrier, inc=1, device_id={'tp': peer}, device_id_type=MESH)
    pl.semaphore_wait(barrier, 3)
    for copy in x_copies + g_copies:
        copy.wait()

    def loop(lo, hi, body):
        lax.fori_loop(lo, hi, lambda i, carry: (body(i), carry)[1], 0)

    def chunks(chunk):
        stats_wait()

        def one(j, first, last):
            ag_wait(j, 0)
            ag_wait(j, 2)
            chunk(j, first, last)

        one(0, True, False)
        forward(2)

        def middle(j):
            one(j, False, False)

            @pl.when(j == 1)
            def _():
                forward(3)

        loop(1, NC - 1, middle)
        one(NC - 1, False, True)

    def layer_body(layer):
        more = layer < LAYERS - 1

        def qkv_chunk(j, first, last):
            for t in range(3):
                wait_tile(layer, 3 * j + t)
            normalize(j, g1_ref, layer)
            block([([(lambda: a_buf[...], slot_of(layer, 3 * j + t))], t, not first, None) for t in range(3)])
            for t in range(3):
                start_up(layer, 3 * j + t + SLOTS - 16)

        chunks(qkv_chunk)
        attention()
        ag_drain()

        def out_tiles(quarters):
            for q in quarters:
                wait_tile(layer, 12 + q)
            block([([(lambda: a_buf[...], slot_of(layer, 12 + q))], q, False, None) for q in quarters])
            for q in quarters:
                rs_a(q)
            for q in quarters:
                refill(layer, 12 + q)

        out_tiles((0,))
        out_tiles((1, 2))
        rs_b(0)
        out_tiles((3,))
        loop(1, NC, rs_b)
        for q in range(NC):
            rs_c(q)
            if q < 2:
                ag_send(q)
        stats_send()
        ag_send(2)
        ag_send(3)
        forward(0)
        forward(1)
        rs_drain()

        def gelu_out(part, q, cols):
            hid[q, :, cols] = jax.nn.gelu(part, approximate=True).astype(jnp.bfloat16)

        def up_chunk(j, first, last):
            for group in ((0,), (1,), (2, 3)) if first else ((0, 1, 2, 3),):
                for q in group:
                    wait_tile(layer, 16 + NC * j + q)
                if group[0] == 0:
                    normalize(j, g2_ref, layer)
                block([([(lambda: a_buf[...], slot_of(layer, 16 + NC * j + q))], q, not first,
                        gelu_out if last else None) for q in group])
                for q in group:
                    if last:
                        refill(layer, 16 + NC * j + q)
                    else:
                        start_down(layer, NC * j + q + SLOTS - 16)

        chunks(up_chunk)
        ag_drain()

        def down_tiles(q, chunk_ids, add):
            for j in chunk_ids:
                wait_tile(layer, 32 + NC * q + j)
            block([([(functools.partial(lambda j: hid[j], j), slot_of(layer, 32 + NC * q + j)) for j in chunk_ids],
                    q, add, None)])

            for k in range(NC):
                if isinstance(q, int):
                    if q == k:
                        for j in chunk_ids:
                            refill(layer, 32 + NC * k + j)
                else:
                    @pl.when(q == k)
                    def _():
                        for j in chunk_ids:
                            refill(layer, 32 + NC * k + j)

        def down_quarter(q):
            down_tiles(q, (0, 1, 2, 3), False)
            rs_a(q)

            @pl.when(q >= 1)
            def _():
                rs_b(q - 1)

        loop(0, NC - 1, down_quarter)
        down_tiles(3, (0, 1), False)
        rs_b(2)
        rs_c(0)

        @pl.when(more)
        def _():
            ag_send(0)

        down_tiles(3, (2,), True)
        down_tiles(3, (3,), True)
        rs_a(3)
        rs_c(1)
        rs_b(3)

        @pl.when(more)
        def _():
            ag_send(1)

        rs_c(2)

        @pl.when(more)
        def _():
            forward(0)

        rs_c(3)

        @pl.when(more)
        def _():
            stats_send()
            ag_send(2)
            ag_send(3)
            forward(1)

        rs_drain()

    ag_send(0)
    for j in range(NC):
        quarter_stats(j)
    stats_send()
    for j in range(1, NC):
        ag_send(j)
    forward(0)
    forward(1)
    loop(0, LAYERS, layer_body)
    y_copies = [pltpu.make_async_copy(x_all.at[j, me], y_hbm.at[0, :, pl.ds(j * C, C)], x_sem.at[j]) for j in range(NC)]
    for copy in y_copies:
        copy.start()
    for copy in y_copies:
        copy.wait()


def solution(mesh):
    def layer_stack(x_local, ln1_gain, w_qkv, w_out, ln2_gain, w_up, w_down):
        w_qkv = jnp.transpose(w_qkv, (0, 2, 1, 3))
        w_out = w_out.reshape(LAYERS, HEADS * HD, D)
        hbm = pl.BlockSpec(memory_space=pl.ANY)
        weight_bytes = 2 * LAYERS * (3 * C * D + C * D + 2 * D * D)
        return pl.pallas_call(
            stack_kernel,
            out_shape=jax.ShapeDtypeStruct(x_local.shape, jnp.bfloat16),
            in_specs=[hbm] * 7,
            out_specs=hbm,
            scratch_shapes=[
                pltpu.VMEM((SLOTS, C, C), jnp.bfloat16),
                pltpu.VMEM((NC, TP, ROWS, C), jnp.bfloat16),
                pltpu.VMEM((SEQ, C), jnp.bfloat16),
                pltpu.VMEM((TP, 8, HD), jnp.float32),
                pltpu.VMEM((NC, 2, ROWS, HD), jnp.float32),
                pltpu.VMEM((SEQ, HD), jnp.float32),
                pltpu.VMEM((SEQ, HD), jnp.float32),
                pltpu.VMEM((NC, SEQ, C), jnp.bfloat16),
                pltpu.VMEM((NC, TP, ROWS, C), jnp.float32),
                pltpu.VMEM((2, 2, ROWS, C), jnp.bfloat16),
                pltpu.VMEM((NC, 2, ROWS, C), jnp.bfloat16),
                pltpu.VMEM((2, ROWS, C), jnp.bfloat16),
                pltpu.VMEM((NC, ROWS, C), jnp.bfloat16),
                pltpu.VMEM((LAYERS, D), jnp.float32),
                pltpu.VMEM((LAYERS, D), jnp.float32),
                pltpu.SemaphoreType.DMA((SLOTS,)),
                pltpu.SemaphoreType.DMA((NC,)),
                pltpu.SemaphoreType.DMA((2,)),
                pltpu.SemaphoreType.DMA((3, NC)),
                pltpu.SemaphoreType.DMA((3, NC)),
                pltpu.SemaphoreType.DMA((3,)),
                pltpu.SemaphoreType.DMA((3,)),
                pltpu.SemaphoreType.DMA((NC,)),
                pltpu.SemaphoreType.DMA((NC,)),
                pltpu.SemaphoreType.DMA((NC,)),
                pltpu.SemaphoreType.DMA((NC,)),
            ],
            compiler_params=pltpu.CompilerParams(collective_id=0, has_side_effects=True, vmem_limit_bytes=67_043_328),
            cost_estimate=pl.CostEstimate(flops=SEQ * weight_bytes, bytes_accessed=weight_bytes, transcendentals=0),
        )(x_local, ln1_gain, w_qkv, w_out, ln2_gain, w_up, w_down)

    return jax.shard_map(layer_stack, mesh=mesh, in_specs=(P('dp', 'tp', None), P(), P(None, None, 'tp', None), P(None, 'tp', None, None), P(), P(None, None, 'tp'), P(None, 'tp', None)), out_specs=P('dp', 'tp', None), check_vma=False)
```

profile of v0, /device:TPU:0, one launch (start us, length us, event | category | flops | bytes accessed | tf_op | source)
XLA Modules:
  0.0 106.8 jit_solution(37649136751251816)
XLA Ops:
  0.0 105.1 %shard_map.73 = bf16[1,32,5120]{2,1,0:T(8,128)(2,1)} custom-call(bf16[1,32,5120]{2,1,0:T(8,128)(2,1)} %x_hbm.1, f32[2,5120]{1,0:T(2,128)} %g1_hbm.1, bf16[2,10,5120,384]{3,2,1,0:T(8,128)(2,1)} %bitcast.wqkv_hbm, bf16[2,1280,5120]{2,1,0:T(8,128)(2,1)} %bitcast.2, f32[2,5120]{1,0:T(2,128)} %g2_hbm.1, bf16[2,5120,5120]{2,1,0:T(8,128)(2,1)} %wup_hbm.1, ...), custom_call_target="tpu_custom_call" | custom-call | flops 40265318400 | bytes 314572800 | tf_op jit(solution)/shard_map/pallas_call | solution.py:417
  105.1 1.7 %copy.9 = bf16[1,32,5120]{2,1,0:T(8,128)(2,1)} copy(bf16[1,32,5120]{2,1,0:T(8,128)(2,1)} %shard_map.73) | data formatting | bytes 655360
where the time goes:
time: 107 us
  Pallas kernels  105 us (98%)
  local copies, waits for them, and re-layouts  1.72 us (2%)
    pallas_call x1, Pallas kernels, layer_stack(): pl.pallas_call(stack_kernel, out_shape=jax.ShapeDtypeStruct(x_local.shape...  105 us

commit v1 on v0

--- a/solution.py
+++ b/solution.py
@@ -283,12 +283,13 @@
                 start_up(layer, 3 * j + t + SLOTS - 16)
 
         chunks(qkv_chunk)
+        wait_tile(layer, 12)
         attention()
-        ag_drain()
 
         def out_tiles(quarters):
             for q in quarters:
-                wait_tile(layer, 12 + q)
+                if q > 0:
+                    wait_tile(layer, 12 + q)
             block([([(lambda: a_buf[...], slot_of(layer, 12 + q))], q, False, None) for q in quarters])
             for q in quarters:
                 rs_a(q)
@@ -297,6 +298,7 @@
 
         out_tiles((0,))
         out_tiles((1, 2))
+        ag_drain()
         rs_b(0)
         out_tiles((3,))
         loop(1, NC, rs_b)
@@ -329,7 +331,6 @@
                         start_down(layer, NC * j + q + SLOTS - 16)
 
         chunks(up_chunk)
-        ag_drain()
 
         def down_tiles(q, chunk_ids, add):
             for j in chunk_ids:
@@ -351,6 +352,10 @@
         def down_quarter(q):
             down_tiles(q, (0, 1, 2, 3), False)
             rs_a(q)
+
+            @pl.when(q == 0)
+            def _():
+                ag_drain()
 
             @pl.when(q >= 1)
             def _():

time: 107 us -> 107 us (level)
  no operation moved by 1% of the time
where the time goes in v1:
time: 107 us
  Pallas kernels  105 us (98%)
  local copies, waits for them, and re-layouts  1.72 us (2%)
    pallas_call x1, Pallas kernels, layer_stack(): pl.pallas_call(stack_kernel, out_shape=jax.ShapeDtypeStruct(x_local.shape...  105 us

profile of v1, /device:TPU:0, one launch (start us, length us, event | category | flops | bytes accessed | tf_op | source)
XLA Modules:
  0.0 106.9 jit_solution(16285137066400201163)
XLA Ops:
  0.0 105.2 %shard_map.73 = bf16[1,32,5120]{2,1,0:T(8,128)(2,1)} custom-call(bf16[1,32,5120]{2,1,0:T(8,128)(2,1)} %x_hbm.1, f32[2,5120]{1,0:T(2,128)} %g1_hbm.1, bf16[2,10,5120,384]{3,2,1,0:T(8,128)(2,1)} %bitcast.wqkv_hbm, bf16[2,1280,5120]{2,1,0:T(8,128)(2,1)} %bitcast.2, f32[2,5120]{1,0:T(2,128)} %g2_hbm.1, bf16[2,5120,5120]{2,1,0:T(8,128)(2,1)} %wup_hbm.1, ...), custom_call_target="tpu_custom_call" | custom-call | flops 40265318400 | bytes 314572800 | tf_op jit(solution)/shard_map/pallas_call | solution.py:422
  105.2 1.7 %copy.9 = bf16[1,32,5120]{2,1,0:T(8,128)(2,1)} copy(bf16[1,32,5120]{2,1,0:T(8,128)(2,1)} %shard_map.73) | data formatting | bytes 655360
